TPU v7x, 32 devices: a whole 2x2x4 slice. The times are simulated.
32 devices in a mesh: pipe: 2 (over x), dp: 4 (over z), tensor: 4 (over y, core).
Axes of the slice: x: 2, y: 2, z: 4, core: 2. Of those that a mesh axis runs over, the one named last changes fastest.
Arguments:
- acts_in: bfloat16 [2, 512, 4096], P(None, 'dp', 'tensor'), may hold values from -6 to 6
- weights: bfloat16 [2, 4096, 4096], P('pipe', None, 'tensor'), may hold values from -0.046875 to 0.046875
- cotangent: bfloat16 [2, 512, 4096], P(None, 'dp', 'tensor'), may hold values from -6 to 6
- hist_act: float32 [2, 16], P('pipe'), may hold values from 2 to 12
- hist_weight: float32 [2, 16], P('pipe'), may hold values from 0.01 to 0.1
- hist_grad: float32 [2, 16], P('pipe'), may hold values from 2 to 12
Outputs:
- section_acts: bfloat16 [2, 2, 512, 4096], P('pipe', None, 'dp', 'tensor')
- section_grads: bfloat16 [2, 2, 512, 4096], P('pipe', None, 'dp', 'tensor')
- weight_grad: bfloat16 [2, 4096, 4096], P('pipe', 'dp', 'tensor')
- new_hist_act: float32 [2, 16], P('pipe')
- new_hist_weight: float32 [2, 16], P('pipe')
- new_hist_grad: float32 [2, 16], P('pipe')
All inputs are finite; a program needn't handle non-finite values.
Results may differ from a plain program's by a relative error of at most 0.025.
Values may be sent and summed in bfloat16 or wider, within the bound.
A program may use at most 128 MiB of HBM per device.

v0:
```python
import functools

import jax
import jax.numpy as jnp
from jax import lax
from jax.experimental import pallas as pl
from jax.experimental.pallas import tpu as pltpu
from jax.sharding import PartitionSpec as P

MESH = pl.DeviceIdType.MESH
PIECES = 2
WIDE = 1024


def strides_below(index, count):
    low = (index & -index) if index else count
    step, found = low // 2, []
    while step:
        found.append(step)
        step //= 2
    return found


def kernel(S, N, T, NC, RC, F, FA,
           acts, weights, cot, hist_a, hist_w, hist_g,
           out_acts, out_grads, out_w, out_top,
           w, xin, xg, xout, acc, gin, part, rs, gout, G, A, dw, dwb, pk, amax, gmax,
           w_sem, x_ss, x_rs, ag_ss, ag_rs, g_ss, g_rs, rd_ss, rd_rs,
           G_ss, G_rs, A_ss, A_rs, B_ss, B_rs, p_ss, p_rs, o_sem, ow_sem):
    s, d, t = lax.axis_index("pipe"), lax.axis_index("dp"), lax.axis_index("tensor")
    last = S - 1
    bf, f32 = jnp.bfloat16, jnp.float32

    def remote(src, dst, ss, rsem, **where):
        return pltpu.make_async_remote_copy(
            src_ref=src, dst_ref=dst, send_sem=ss, recv_sem=rsem,
            device_id=where, device_id_type=MESH)

    loads = [pltpu.make_async_copy(weights.at[b], w.at[b], w_sem.at[b]) for b in range(T)]
    for copy in loads:
        copy.start()

    barrier = pltpu.get_barrier_semaphore()
    for k in range(N):
        for j in range(T):
            if k or j:
                pl.semaphore_signal(barrier, inc=1, device_id={"dp": d ^ k, "tensor": t ^ j},
                                    device_id_type=MESH)

    @pl.when(s > 0)
    def _():
        pl.semaphore_signal(barrier, inc=1, device_id={"pipe": s - 1}, device_id_type=MESH)

    @pl.when(s < last)
    def _():
        pl.semaphore_signal(barrier, inc=1, device_id={"pipe": s + 1}, device_id_type=MESH)

    lim_a = jnp.max(hist_a[...], axis=1, keepdims=True).astype(bf)
    lim_w = jnp.max(hist_w[...], axis=1, keepdims=True).astype(bf)
    lim_g = jnp.max(hist_g[...], axis=1, keepdims=True).astype(bf)

    def clip(v, lim):
        return jnp.minimum(jnp.maximum(v, -lim), lim)

    def fold(v):
        return jnp.max(jnp.abs(v).reshape(-1, 16, v.shape[-1]), axis=0)

    amax[...] = jnp.zeros_like(amax)
    gmax[...] = jnp.zeros_like(gmax)

    near = (s > 0).astype(jnp.int32) + (s < last).astype(jnp.int32)
    pl.semaphore_wait(barrier, N * T - 1 + near)

    up = jnp.minimum(s + 1, last)
    down = jnp.maximum(s - 1, 0)

    def x_copy(c):
        return remote(xout.at[c], xin.at[c], x_ss.at[c], x_rs.at[c], pipe=up)

    def g_copy(c):
        return remote(gout.at[c], gin.at[c], g_ss.at[c], g_rs.at[c], pipe=down)

    def ag_copy(c, j, st):
        i = j ^ st
        return remote(xg.at[c, j], xg.at[c, i], ag_ss.at[c, i], ag_rs.at[c, i], tensor=t ^ st)

    def low(i):
        return i & -i

    def G_copy(c, j, st):
        i = j ^ st
        return remote(G.at[c, j], G.at[c, i], G_ss.at[c, i], G_rs.at[c, i], dp=d ^ st)

    ratio = N // T

    def in_block(r):
        start = lax.rem(r, ratio) * FA
        return t ^ lax.div(r, ratio), pl.ds(pl.multiple_of(start, FA), FA)

    piece = RC // T

    def rows_of(owner):
        return pl.ds(pl.multiple_of(owner * piece, piece), piece)

    def A_copy(c, k):
        owner, cols = in_block(d ^ k)
        return remote(xg.at[c, owner, rows_of(t), cols], A.at[c, k, rows_of(t)],
                      A_ss.at[c, k], A_rs.at[c, k], dp=d ^ k)

    def B_copy(c, j, st):
        i = j ^ st
        there = A.at[c, pl.ds(1, N - 1), rows_of(t ^ j)]
        return remote(there, there, B_ss.at[c, i], B_rs.at[c, i], tensor=t ^ st)

    def B_arrival(c, i):
        there = A.at[c, pl.ds(1, N - 1), rows_of(t ^ i)]
        return remote(there, there, B_ss.at[c, i], B_rs.at[c, i], tensor=t ^ low(i))

    stages = []
    st = 1
    while st < T:
        stages.append(st)
        st *= 2

    def rd_copy(c, j, level):
        st = stages[level]
        i = j ^ st
        return remote(part.at[c, j], rs.at[c, level, i], rd_ss.at[c, j], rd_rs.at[c, level, i],
                      tensor=t ^ st)

    def prep(c):
        @pl.when(s == 0)
        def _():
            xin[c] = acts[c]

        @pl.when(s > 0)
        def _():
            x_copy(c).wait_recv()

        x = xin[c]
        xg[c, 0] = clip(x, lim_a)
        for st in strides_below(0, T):
            ag_copy(c, 0, st).start()
        amax[...] = jnp.maximum(amax[...], fold(x))

    def clip_weights():
        peak = jnp.zeros((16, F), bf)
        for b in range(T):
            loads[b].wait()

            def body(i, m, b=b):
                rows = pl.ds(pl.multiple_of(i * 128, 128), 128)
                v = w[b, rows]
                w[b, rows] = clip(v, lim_w)
                return jnp.maximum(m, fold(v))

            peak = lax.fori_loop(0, F // 128, body, peak)
        return jnp.max(peak.astype(f32), keepdims=True).reshape(1, 1)

    def compute(c):
        for j in range(T):
            if j:
                ag_copy(c, j ^ low(j), low(j)).wait_recv()
                for st in strides_below(j, T):
                    ag_copy(c, j, st).start()
            b = t ^ j

            def body(n, _, j=j, b=b):
                cols = pl.ds(pl.multiple_of(n * WIDE, WIDE), WIDE)
                y = jnp.dot(xg[c, j], w[b, :, cols], preferred_element_type=f32)
                if j == 0:
                    acc[:, cols] = y
                elif j < T - 1:
                    acc[:, cols] += y
                else:
                    xout[c, :, cols] = (acc[:, cols] + y + xin[c, :, cols].astype(f32)).astype(bf)
                return 0

            lax.fori_loop(0, F // WIDE, body, 0)

        @pl.when(s < last)
        def _():
            x_copy(c).start()

        pltpu.make_async_copy(xout.at[c], out_acts.at[c], o_sem.at[0, c]).start()
        for k in range(1, N):
            A_copy(c, k).start()
        owner, cols = in_block(d)
        A[c, 0] = xg[c, owner, :, cols]

    def prepb(c, is_last):
        if is_last:
            gin[c] = (cot[c].astype(f32) * xout[c].astype(f32)).astype(bf)
        else:
            g_copy(c).wait_recv()
        g = gin[c]
        G[c, 0] = clip(g, lim_g)
        for st in strides_below(0, N):
            G_copy(c, 0, st).start()
        gmax[...] = jnp.maximum(gmax[...], fold(g))
        order = sorted(range(T), key=lambda j: -(low(j) == 1))
        for j in order:
            b = t ^ j

            def body(n, _, j=j, b=b):
                cols = pl.ds(pl.multiple_of(n * WIDE, WIDE), WIDE)
                y = lax.dot_general(G[c, 0], w[b, cols, :], (((1,), (1,)), ((), ())),
                                    preferred_element_type=f32)
                part[c, j, :, cols] = y.astype(bf)
                return 0

            lax.fori_loop(0, F // WIDE, body, 0)
            if low(j) == 1:
                rd_copy(c, j, 0).start()

    def midb(c):
        for level in range(len(stages) - 1):
            st = stages[level]
            js = list(range(0, T, 2 * st))
            for j in sorted(js, key=lambda j: -(low(j) == 2 * st)):
                if j == 0:
                    continue
                rd_copy(c, j ^ st, level).wait_recv()
                part[c, j] = (part[c, j].astype(f32) + rs[c, level, j].astype(f32)).astype(bf)
                if low(j) == 2 * st:
                    rd_copy(c, j, level + 1).start()

    def finb(c):
        total = gin[c].astype(f32) + part[c, 0].astype(f32)
        for level in range(len(stages)):
            rd_copy(c, stages[level], level).wait_recv()
            total = total + rs[c, level, 0].astype(f32)
        gout[c] = total.astype(bf)

        @pl.when(s > 0)
        def _():
            g_copy(c).start()

        pltpu.make_async_copy(gout.at[c], out_grads.at[c], o_sem.at[1, c]).start()

    def relay_G(c):
        for j in range(1, N):
            if strides_below(j, N):
                G_copy(c, j ^ low(j), low(j)).wait_recv()
                for st in strides_below(j, N):
                    G_copy(c, j, st).start()

    def relay_A(c):
        for k in range(1, N):
            A_copy(c, k).wait_recv()
        for st in strides_below(0, T):
            B_copy(c, 0, st).start()

    def relay_B(c):
        for j in range(1, T):
            if strides_below(j, T):
                B_arrival(c, j).wait_recv()
                for st in strides_below(j, T):
                    B_copy(c, j, st).start()

    def update(c):
        for j in range(1, N):
            if not strides_below(j, N):
                G_copy(c, j ^ low(j), low(j)).wait_recv()
        for j in range(1, T):
            if not strides_below(j, T):
                B_arrival(c, j).wait_recv()
        tile = 256

        def body(n, _):
            cols = pl.ds(pl.multiple_of(n * tile, tile), tile)
            y = lax.dot_general(A[c, :, :, cols].reshape(N * RC, tile), G[c].reshape(N * RC, F),
                                (((0,), (0,)), ((), ())), preferred_element_type=f32)
            if c == 0:
                dw[cols, :] = y
            elif c < NC - 1:
                dw[cols, :] += y
            else:
                dwb[cols, :] = (dw[cols, :] + y).astype(bf)
            return 0

        lax.fori_loop(0, FA // tile, body, 0)

    def peers():
        return [(k, j) for k in range(N) for j in range(T) if k or j]

    def p_copy(k, j):
        i = k * T + j
        return remote(pk.at[0], pk.at[i], p_ss.at[i], p_rs.at[i], dp=d ^ k, tensor=t ^ j)

    def send_peaks():
        row = lax.broadcasted_iota(jnp.int32, (8, 128), 0)
        top_a = jnp.max(amax[...].astype(f32), keepdims=True).reshape(1, 1)
        top_g = jnp.max(gmax[...].astype(f32), keepdims=True).reshape(1, 1)
        pk[0] = jnp.where(row == 0, top_a, jnp.where(row == 1, w_peak, top_g))
        for k, j in peers():
            p_copy(k, j).start()

    prep(0)
    if NC > 1:
        prep(1)
    w_peak = clip_weights()

    def backward(i, is_last):
        if i < NC:
            prepb(i, is_last)
            if i == NC - 1:
                send_peaks()
            midb(i)
        if 1 <= i <= NC:
            finb(i - 1)

    @pl.when(s == last)
    def _():
        for c in range(NC):
            compute(c)
            if c + 2 < NC:
                prep(c + 2)
            backward(c, True)
        backward(NC, True)
        for c in range(NC):
            relay_A(c)
            relay_G(c)
        for c in range(NC):
            relay_B(c)
        for c in range(NC - 1):
            update(c)

    @pl.when(s < last)
    def _():
        for c in range(NC):
            compute(c)
            if c + 2 < NC:
                prep(c + 2)
        for c in range(NC):
            relay_A(c)
        for c in range(NC):
            relay_B(c)
        for c in range(NC + 1):
            backward(c, False)
            if c >= 1:
                relay_G(c - 1)
            if c >= 3:
                update(c - 3)
        for c in range(NC - 2, NC - 1):
            update(c)

    update(NC - 1)
    out = pltpu.make_async_copy(dwb, out_w, ow_sem)
    out.start()

    for k, j in peers():
        p_copy(k, j).wait_recv()
    top = jnp.max(pk[...], axis=0)
    out_top[...] = top

    for c in range(NC):
        for i in range(1, T):
            ag_copy(c, i ^ low(i), low(i)).wait_send()
        for level, st in enumerate(stages):
            for j in range(0, T, st):
                if j & st:
                    rd_copy(c, j, level).wait_send()
        for i in range(1, N):
            G_copy(c, i ^ low(i), low(i)).wait_send()
            A_copy(c, i).wait_send()
        for i in range(1, T):
            B_copy(c, i ^ low(i), low(i)).wait_send()
        pltpu.make_async_copy(xout.at[c], out_acts.at[c], o_sem.at[0, c]).wait()
        pltpu.make_async_copy(gout.at[c], out_grads.at[c], o_sem.at[1, c]).wait()

        @pl.when(s < last)
        def _():
            x_copy(c).wait_send()

        @pl.when(s > 0)
        def _():
            g_copy(c).wait_send()

    for k, j in peers():
        p_copy(k, j).wait_send()
    out.wait()


def finish(acts, grads, dw, top, hist_a, hist_w, hist_g,
           out_acts, out_grads, out_w, out_ha, out_hw, out_hg, held_a, held_g, held_w, in_sem, out_sem):
    half = dw.shape[0] // 2
    moves = [(acts, held_a, out_acts.at[0]), (grads, held_g, out_grads.at[0])]
    for i in range(2):
        rows = pl.ds(i * half, half)
        moves.append((dw.at[rows], held_w.at[rows], out_w.at[0, rows]))
    inward = [pltpu.make_async_copy(src, held, in_sem.at[0, i]) for i, (src, held, _) in enumerate(moves)]
    outward = [pltpu.make_async_copy(held, dst, out_sem.at[0, i]) for i, (_, held, dst) in enumerate(moves)]
    for copy in inward:
        copy.start()
    peaks = top[...]
    for row, (hist, out_hist) in enumerate(((hist_a, out_ha), (hist_w, out_hw), (hist_g, out_hg))):
        old = hist[...]
        out_hist[...] = jnp.concatenate([peaks[row:row + 1, 0:1], old[:, :-1]], axis=1)
    for copy, onward in zip(inward, outward):
        copy.wait()
        onward.start()
    for onward in outward:
        onward.wait()


def shards(acts_in, weights, cotangent, hist_act, hist_weight, hist_grad):
    S, N, T = lax.axis_size("pipe"), lax.axis_size("dp"), lax.axis_size("tensor")
    M, R, F = acts_in.shape
    NC, RC = M * PIECES, R // PIECES
    FA = T * F // N
    bf, f32 = jnp.bfloat16, jnp.float32
    levels = max(1, T.bit_length() - 1)
    dma = pltpu.SemaphoreType.DMA
    vmem = pl.BlockSpec(memory_space=pltpu.VMEM)
    anyw = pl.BlockSpec(memory_space=pl.ANY)
    hist = jax.ShapeDtypeStruct(hist_act.shape, f32)
    chunk = (NC, RC, F)
    acts, grads, dw, top = pl.pallas_call(
        functools.partial(kernel, S, N, T, NC, RC, F, FA),
        out_shape=(jax.ShapeDtypeStruct(chunk, bf), jax.ShapeDtypeStruct(chunk, bf),
                   jax.ShapeDtypeStruct((FA, F), bf), jax.ShapeDtypeStruct((8, 128), f32)),
        in_specs=[vmem, anyw, vmem, vmem, vmem, vmem],
        out_specs=(anyw, anyw, anyw, vmem),
        scratch_shapes=[
            pltpu.VMEM((T, F, F), bf),
            pltpu.VMEM(chunk, bf),
            pltpu.VMEM((NC, T, RC, F), bf),
            pltpu.VMEM(chunk, bf),
            pltpu.VMEM((RC, F), f32),
            pltpu.VMEM(chunk, bf),
            pltpu.VMEM((NC, T, RC, F), bf),
            pltpu.VMEM((NC, levels, T, RC, F), bf),
            pltpu.VMEM(chunk, bf),
            pltpu.VMEM((NC, N, RC, F), bf),
            pltpu.VMEM((NC, N, RC, FA), bf),
            pltpu.VMEM((FA, F), f32),
            pltpu.VMEM((FA, F), bf),
            pltpu.VMEM((N * T, 8, 128), f32),
            pltpu.VMEM((16, F), bf),
            pltpu.VMEM((16, F), bf),
            dma((T,)), dma((NC,)), dma((NC,)), dma((NC, T)), dma((NC, T)),
            dma((NC,)), dma((NC,)), dma((NC, T)), dma((NC, levels, T)),
            dma((NC, N)), dma((NC, N)), dma((NC, N)), dma((NC, N)), dma((NC, T)), dma((NC, T)),
            dma((N * T,)), dma((N * T,)), dma((2, NC)), dma(()),
        ],
        compiler_params=pltpu.CompilerParams(
            collective_id=0, has_side_effects=True, vmem_limit_bytes=60 * 2**20),
    )(acts_in.reshape(chunk), weights.reshape(T, F, F), cotangent.reshape(chunk),
      hist_act, hist_weight, hist_grad)
    full = (1, M, R, F)
    return pl.pallas_call(
        finish,
        out_shape=(jax.ShapeDtypeStruct(full, bf), jax.ShapeDtypeStruct(full, bf),
                   jax.ShapeDtypeStruct((1, FA, F), bf), hist, hist, hist),
        in_specs=[anyw, anyw, anyw, vmem, vmem, vmem, vmem],
        out_specs=(anyw, anyw, anyw, vmem, vmem, vmem),
        scratch_shapes=[pltpu.VMEM((M, R, F), bf), pltpu.VMEM((M, R, F), bf),
                        pltpu.VMEM((FA, F), bf), dma((2, 4)), dma((2, 4))],
        compiler_params=pltpu.CompilerParams(vmem_limit_bytes=60 * 2**20),
    )(acts.reshape(M, R, F), grads.reshape(M, R, F), dw, top, hist_act, hist_weight, hist_grad)


def solution(mesh):
    placed = (P(None, "dp", "tensor"), P("pipe", None, "tensor"), P(None, "dp", "tensor"),
              P("pipe", None), P("pipe", None), P("pipe", None))
    return jax.shard_map(
        shards, mesh=mesh, in_specs=placed,
        out_specs=(P("pipe", None, "dp", "tensor"), P("pipe", None, "dp", "tensor"),
                   P("pipe", "dp", "tensor"), P("pipe", None), P("pipe", None), P("pipe", None)),
        check_vma=False)
```

profile of v0, /device:TPU:0, one launch (start us, length us, event | category | flops | bytes accessed | tf_op | source)
XLA Modules:
  0.0 85.3 jit_solution(3231495940238860750)
XLA Ops:
  0.6 80.2 %shard_map.109 = (bf16[4,64,1024]{2,1,0:T(8,128)(2,1)}, bf16[4,64,1024]{2,1,0:T(8,128)(2,1)}, bf16[1024,1024]{1,0:T(8,128)(2,1)}, f32[8,128]{1,0:T(8,128)}) custom-call(bf16[4,64,1024]{2,1,0:T(8,128)(2,1)} %bitcast.6, bf16[4,1024,1024]{2,1,0:T(8,128)(2,1)} %bitcast.5, bf16[4,64,1024]{2,1,0:T(8,128)(2,1)} %bitcast.7, f32[1,16]{1,0:T(1,128)} %hist_a.3, ...), custom_call_target="tpu_custom_call" | custom-call | tf_op jit(solution)/shard_map/pallas_call | solution.py:419
  80.9 4.2 %shard_map.110 = (bf16[1,2,128,1024]{3,2,1,0:T(8,128)(2,1)}, bf16[1,2,128,1024]{3,2,1,0:T(8,128)(2,1)}, bf16[1,1024,1024]{2,1,0:T(8,128)(2,1)}, f32[1,16]{1,0:T(...) custom-call(bf16[2,128,1024]{2,1,0:T(8,128)(2,1)} %bitcast.8, bf16[2,128,1024]{2,1,0:T(8,128)(2,1)} %bitcast.9, ...), custom_call_target="tpu_custom_call" | custom-call | tf_op jit(solution)/shard_map/pallas_call | solution.py:452
where the time goes:
time: 85.4 us; the launch traced here: 85.3 us
  Pallas kernels  84.4 us (99%)
    pallas_call x1, Pallas kernels, shards(): pl.pallas_call(functools.partial(kernel, S, N, T, NC, RC, F, FA), out_sha...  80.2 us
    pallas_call x1, Pallas kernels, shards(): pl.pallas_call(finish, out_shape=(jax.ShapeDtypeStruct(full, bf), jax.Sha...  4.22 us

commit v1 on v0

v1 whole, which is shorter than its diff:
```python
import functools

import jax
import jax.numpy as jnp
from jax import lax
from jax.experimental import pallas as pl
from jax.experimental.pallas import tpu as pltpu
from jax.sharding import PartitionSpec as P

MESH = pl.DeviceIdType.MESH
FIRST, LATER = (4, 4, 2), (2, 2)


def strides_below(index, count):
    low = (index & -index) if index else count
    step, found = low // 2, []
    while step:
        found.append(step)
        step //= 2
    return found


def low(i):
    return i & -i


def chunks_of(M, R):
    found = []
    for m in range(M):
        start = 0
        for part in FIRST if m == 0 else LATER:
            found.append((m, start, R // part))
            start += R // part
    return found


def kernel(S, N, T, M, R, F, FA, chunks,
           acts, weights, cot, hist_a, hist_w, hist_g,
           xout, gout, G, At, dw, out_top,
           w, wt, hv, cv, xin, xg, acc, gin, part, rs, A, pk, amax, gmax,
           w_sem, h_sem, in_sem, c_sem, x_ss, x_rs, ag_ss, ag_rs, g_ss, g_rs, rd_ss, rd_rs,
           G_ss, G_rs, Gr_ss, A_ss, A_rs, B_ss, B_rs, p_ss, p_rs, hello):
    s, d, t = lax.axis_index("pipe"), lax.axis_index("dp"), lax.axis_index("tensor")
    last = S - 1
    bf, f32 = jnp.bfloat16, jnp.float32
    NC = len(chunks)
    stages = []
    st = 1
    while st < T:
        stages.append(st)
        st *= 2

    def remote(src, dst, ss, rsem, **where):
        return pltpu.make_async_remote_copy(
            src_ref=src, dst_ref=dst, send_sem=ss, recv_sem=rsem,
            device_id=where, device_id_type=MESH)

    def signal(sem, **where):
        pl.semaphore_signal(sem, inc=1, device_id=where, device_id_type=MESH)

    barrier = pltpu.get_barrier_semaphore()
    for st in stages:
        signal(barrier, tensor=t ^ st)

    @pl.when(s > 0)
    def _():
        signal(barrier, pipe=s - 1)

    @pl.when(s < last)
    def _():
        signal(barrier, pipe=s + 1)

    @pl.when(d > 0)
    def _():
        signal(barrier, dp=d - 1)

    @pl.when(d < N - 1)
    def _():
        signal(barrier, dp=d + 1)

    def rows_at(c):
        m, start, n = chunks[c]
        return pl.ds(m * R + start, n)

    h_loads = [pltpu.make_async_copy(h, hv.at[i], h_sem)
               for i, h in enumerate((hist_a, hist_w, hist_g))]
    loads = [pltpu.make_async_copy(weights.at[b], w.at[b], w_sem.at[b]) for b in range(T)]
    first = chunks[0][2]
    in_loads = [pltpu.make_async_copy(acts.at[rows], xin.at[rows], in_sem.at[i])
                for i, rows in enumerate((pl.ds(0, first), pl.ds(first, M * R - first)))]
    cot_load = pltpu.make_async_copy(cot, cv, c_sem)
    for copy in h_loads:
        copy.start()

    @pl.when(s == 0)
    def _():
        for copy in in_loads:
            copy.start()

    pltpu.make_async_copy(hv, hv, h_sem).wait()
    for copy in loads:
        copy.start()

    @pl.when(s == last)
    def _():
        cot_load.start()

    def limit(i):
        return jnp.max(hv[i], axis=1, keepdims=True).astype(bf)

    lim_a, lim_w, lim_g = limit(0), limit(1), limit(2)

    def clip(v, lim):
        return jnp.minimum(jnp.maximum(v, -lim), lim)

    def fold(v):
        return jnp.max(jnp.abs(v).reshape(-1, 16, v.shape[-1]), axis=0)

    amax[...] = jnp.zeros_like(amax)
    gmax[...] = jnp.zeros_like(gmax)

    def enter():
        near = (s > 0).astype(jnp.int32) + (s < last).astype(jnp.int32)
        beside = (d > 0).astype(jnp.int32) + (d < N - 1).astype(jnp.int32)
        pl.semaphore_wait(barrier, len(stages) + near + beside)

    def greet(r):
        @pl.when(d > 0)
        def _():
            signal(hello.at[r, 0], dp=d - 1)

        @pl.when(d < N - 1)
        def _():
            signal(hello.at[r, 1], dp=d + 1)

    def greeted(r):
        @pl.when(d < N - 1)
        def _():
            pl.semaphore_wait(hello.at[r, 0], 1)

        @pl.when(d > 0)
        def _():
            pl.semaphore_wait(hello.at[r, 1], 1)

    up = jnp.minimum(s + 1, last)
    down = jnp.maximum(s - 1, 0)

    def x_copy(c):
        return remote(xout.at[rows_at(c)], xin.at[rows_at(c)], x_ss, x_rs.at[c], pipe=up)

    def g_copy(c):
        return remote(gout.at[rows_at(c)], gin.at[rows_at(c)], g_ss, g_rs.at[c], pipe=down)

    def ag_copy(c, j, st):
        i = j ^ st
        return remote(xg.at[j, rows_at(c)], xg.at[i, rows_at(c)], ag_ss, ag_rs.at[c, i - 1], tensor=t ^ st)

    def G_copy(c, origin, to, ss):
        m, start, n = chunks[c]
        rows = pl.ds(start, n)
        return remote(G.at[m, origin ^ d, rows], G.at[m, origin ^ to, rows], ss, G_rs.at[c, (origin ^ to) - 1], dp=to)

    def G_wait(c, origin):
        m, start, n = chunks[c]
        here = G.at[m, origin ^ d, pl.ds(start, n)]
        remote(here, here, G_ss.at[0], G_rs.at[c, (origin ^ d) - 1], dp=origin).wait_recv()

    def inside(at):
        return (at >= 0) & (at < N)

    def own_sends(act):
        for i, step in enumerate((1, -1, 2, -2)):
            if abs(step) < N:
                @pl.when(inside(d + step))
                def _(i=i, to=d + step):
                    act(to, G_ss.at[i])

    def relays(wait, act):
        for i, way in enumerate((1, -1)):
            for m in range(1, (N + 1) // 2):
                origin = d - way * 2 * m

                @pl.when(inside(origin) & inside(d + way))
                def _(i=i, way=way, m=m, origin=origin):
                    wait(origin)
                    for step in (1, 2):
                        if 2 * m + step < N:
                            @pl.when(inside(d + way * step))
                            def _(step=step):
                                act(origin, d + way * step, Gr_ss.at[i, m - 1, step - 1])

    ratio = N // T

    def in_block(r):
        start = lax.rem(r, ratio) * FA
        return t ^ lax.div(r, ratio), pl.ds(pl.multiple_of(start, FA), FA)

    piece = R // T

    def rows_of(owner):
        return pl.ds(pl.multiple_of(owner * piece, piece), piece)

    def A_copy(m, k):
        owner, cols = in_block(d ^ k)
        src = pl.ds(pl.multiple_of(m * R + t * piece, piece), piece)
        return remote(xg.at[owner, src, cols], A.at[m, k, rows_of(t)],
                      A_ss, A_rs.at[m], dp=d ^ k)

    def B_copy(m, j, st):
        i = j ^ st
        there = A.at[m, pl.ds(1, N - 1), rows_of(t ^ j)]
        return remote(there, there, B_ss, B_rs.at[m, i - 1], tensor=t ^ st)

    def B_arrival(m, i):
        there = A.at[m, pl.ds(1, N - 1), rows_of(t ^ i)]
        return remote(there, there, B_ss, B_rs.at[m, i - 1], tensor=t ^ low(i))

    def rd_copy(c, j, level):
        st = stages[level]
        i = j ^ st
        return remote(part.at[j, rows_at(c)], rs.at[level, i, rows_at(c)], rd_ss, rd_rs.at[c, i + st - 1],
                      tensor=t ^ st)

    def prep(c):
        rows = rows_at(c)

        @pl.when(s == 0)
        def _():
            if c < len(in_loads):
                in_loads[c].wait()

        @pl.when(s > 0)
        def _():
            x_copy(c).wait_recv()

        x = xin[rows]
        xg[0, rows] = clip(x, lim_a)
        for st in strides_below(0, T):
            ag_copy(c, 0, st).start()
        amax[...] = jnp.maximum(amax[...], fold(x))

    def clip_weights():
        peak = jnp.zeros((16, F), bf)
        for b in range(T):
            loads[b].wait()

            def body(i, m, b=b):
                rows = pl.ds(pl.multiple_of(i * 128, 128), 128)
                v = w[b, rows]
                w[b, rows] = clip(v, lim_w)
                return jnp.maximum(m, fold(v))

            peak = lax.fori_loop(0, F // 128, body, peak)
        return jnp.max(peak.astype(f32), keepdims=True).reshape(1, 1)

    def turn_weights():
        for b in range(T):
            def body(i, _, b=b):
                rows = pl.ds(pl.multiple_of(i * 128, 128), 128)
                wt[b, :, rows] = w[b, rows].T
                return 0

            lax.fori_loop(0, F // 128, body, 0)

    def fwd(c):
        rows = rows_at(c)
        n = chunks[c][2]

        def term(j):
            return jnp.dot(xg[j, rows], w[t ^ j], preferred_element_type=f32)

        for j in range(T):
            if j:
                ag_copy(c, j ^ low(j), low(j)).wait_recv()
                for st in strides_below(j, T):
                    ag_copy(c, j, st).start()
            if j == 0:
                if T == 1:
                    xout[rows] = (term(0) + xin[rows].astype(f32)).astype(bf)
            elif j == 1:
                y = term(0) + term(1)
                if T == 2:
                    xout[rows] = (y + xin[rows].astype(f32)).astype(bf)
                else:
                    acc[:n] = y
            elif j < T - 1:
                acc[:n] += term(j)
            else:
                xout[rows] = (acc[:n] + term(j) + xin[rows].astype(f32)).astype(bf)

        @pl.when(s < last)
        def _():
            x_copy(c).start()

    def send_A(m):
        for k in range(1, N):
            A_copy(m, k).start()
        owner, cols = in_block(d)
        A[m, 0] = xg[owner, pl.ds(m * R, R), cols]

    def bwd(c, is_last):
        m, start, n = chunks[c]
        rows = rows_at(c)
        if is_last:
            gin[rows] = (cv[rows].astype(f32) * xout[rows].astype(f32)).astype(bf)
        else:
            g_copy(c).wait_recv()
        g = gin[rows]
        G[m, 0, pl.ds(start, n)] = clip(g, lim_g)
        own_sends(lambda to, ss: G_copy(c, d, to, ss).start())
        gmax[...] = jnp.maximum(gmax[...], fold(g))

        def settle(j):
            level = 0
            while not (j >> level) & 1:
                rd_copy(c, j ^ stages[level], level).wait_recv()
                part[j, rows] = (part[j, rows].astype(f32) + rs[level, j, rows].astype(f32)).astype(bf)
                level += 1
            rd_copy(c, j, level).start()

        for j in reversed(range(T)):
            y = jnp.dot(G[m, 0, pl.ds(start, n)], wt[t ^ j], preferred_element_type=f32)
            part[j, rows] = y.astype(bf)
            if j & 1:
                rd_copy(c, j, 0).start()
                if j + 1 < T:
                    settle(j + 1)

    def finb(c):
        rows = rows_at(c)
        total = gin[rows].astype(f32) + part[0, rows].astype(f32)
        for level in range(len(stages)):
            rd_copy(c, stages[level], level).wait_recv()
            total = total + rs[level, 0, rows].astype(f32)
        gout[rows] = total.astype(bf)

        @pl.when(s > 0)
        def _():
            g_copy(c).start()

    def relay_G(c):
        relays(lambda origin: G_wait(c, origin), lambda origin, to, ss: G_copy(c, origin, to, ss).start())

    def arrive_G(c):
        for step in range(1, N):
            for way in (1, -1):
                origin = d - way * step
                here = inside(origin)
                if step % 2 == 0:
                    here = here & ~inside(d + way)

                @pl.when(here)
                def _(origin=origin):
                    G_wait(c, origin)

    def relay_A(m):
        there = A.at[m, pl.ds(1, N - 1), rows_of(t)]
        remote(there, there, A_ss, A_rs.at[m], dp=d ^ 1).wait_recv()
        for st in strides_below(0, T):
            B_copy(m, 0, st).start()

    def relay_B(m):
        for j in range(1, T):
            if strides_below(j, T):
                B_arrival(m, j).wait_recv()
                for st in strides_below(j, T):
                    B_copy(m, j, st).start()

    def turn_A(m):
        for j in range(1, T):
            if not strides_below(j, T):
                B_arrival(m, j).wait_recv()
        for k in range(N):
            def body(i, _, k=k):
                cols = pl.ds(pl.multiple_of(i * 128, 128), 128)
                At[m, cols, pl.ds(k * R, R)] = A[m, k, :, cols].T
                return 0

            lax.fori_loop(0, FA // 128, body, 0)

    def update(m):
        def body(n, _):
            rows = pl.ds(pl.multiple_of(n * 128, 128), 128)
            y = jnp.dot(At[m, rows], G[m].reshape(N * R, F), preferred_element_type=f32)
            if m == 0:
                dw[rows] = y
            else:
                dw[rows] += y
            return 0

        lax.fori_loop(0, FA // 128, body, 0)

    def peers():
        return [(k, j) for k in range(N) for j in range(T) if k or j]

    def p_copy(k, j):
        i = k * T + j
        return remote(pk.at[0], pk.at[i], p_ss, p_rs, dp=d ^ k, tensor=t ^ j)

    def send_peaks():
        row = lax.broadcasted_iota(jnp.int32, (8, 128), 0)
        top_a = jnp.max(amax[...].astype(f32), keepdims=True).reshape(1, 1)
        top_g = jnp.max(gmax[...].astype(f32), keepdims=True).reshape(1, 1)
        pk[0] = jnp.where(row == 0, top_a, jnp.where(row == 1, w_peak, top_g))
        for k, j in peers():
            p_copy(k, j).start()

    ends = [max(c for c in range(NC) if chunks[c][0] == m) for m in range(M)]

    def meet(first, end):
        for r in range(first, end):
            greeted(r)
            if r + 1 < N - 2:
                greet(r + 1)

    enter()
    greet(0)

    @pl.when(s == 0)
    def _():
        prep(0)
        prep(1)

    w_peak = clip_weights()

    @pl.when(s > 0)
    def _():
        turn_weights()
        meet(0, N - 2)
        prep(0)
        prep(1)

    def arrive(m):
        for c in range(NC):
            if chunks[c][0] == m:
                arrive_G(c)

    @pl.when(s == last)
    def _():
        cot_load.wait()
        for c in range(NC):
            fwd(c)
            if c in ends:
                send_A(ends.index(c))
            bwd(c, True)
            if c == NC - 1:
                send_peaks()
            if c + 2 < NC:
                prep(c + 2)
            if c:
                finb(c - 1)
            if c >= 2:
                relay_G(c - 2)
        finb(NC - 1)
        for m in range(M - 1):
            relay_A(m)
        relay_G(NC - 2)
        relay_A(M - 1)
        for m in range(M - 1):
            relay_B(m)
            turn_A(m)
            arrive(m)
            update(m)
        relay_B(M - 1)
        relay_G(NC - 1)
        turn_A(M - 1)

    @pl.when(s < last)
    def _():
        for c in range(NC):
            fwd(c)
            if c + 2 < NC:
                prep(c + 2)
            if c < 2:
                @pl.when(s == 0)
                def _(c=c):
                    meet(max(0, N - 3) * c, N - 3 + c)
            if c in ends:
                send_A(ends.index(c))

        @pl.when(s == 0)
        def _():
            turn_weights()

        relay_A(0)
        for c in range(NC):
            bwd(c, False)
            if c == NC - 1:
                send_peaks()
            if c:
                finb(c - 1)
            if c < M - 1:
                relay_A(c + 1)
            if 1 <= c <= M:
                relay_B(c - 1)
            if c >= 2:
                relay_G(c - 2)
            if 2 <= c < M + 2:
                turn_A(c - 2)
        relay_G(NC - 2)
        finb(NC - 1)
        for m in range(M - 1):
            arrive(m)
            update(m)
        relay_G(NC - 1)

    arrive(M - 1)

    def peakwait():
        there = pk.at[pl.ds(1, N * T - 1)]
        remote(there, there, p_ss, p_rs, dp=d ^ 1).wait_recv()
        out_top[...] = jnp.max(pk[...], axis=0)

    def sent(ref, sem):
        remote(ref, ref, sem, p_rs, dp=d ^ 1).wait_send()

    def finalwait():
        most = pl.ds(0, T - 1)
        sent(xg.at[most], ag_ss)
        sent(part.at[most], rd_ss)
        own_sends(lambda to, ss: sent(gin, ss))
        relays(lambda origin: None, lambda origin, to, ss: sent(gin, ss))

        @pl.when(s < last)
        def _():
            sent(gin, x_ss)

        @pl.when(s > 0)
        def _():
            sent(gin, g_ss)

        sent(A.at[:, pl.ds(1, N - 1), rows_of(t)], A_ss)
        sent(A.at[:, pl.ds(1, N - 1), pl.ds(0, (T - 1) * piece)], B_ss)
        sent(pk.at[pl.ds(1, N * T - 1)], p_ss)

    peakwait()
    finalwait()


def finish(M, tile, acts, grads, G, At, dw, top, hist_a, hist_w, hist_g,
           out_acts, out_grads, out_w, out_ha, out_hw, out_hg, held, hv, hn, sem, w_sem, h_sem, n_sem):
    moves = [pltpu.make_async_copy(acts, out_acts, sem.at[0]),
             pltpu.make_async_copy(grads, out_grads, sem.at[1])]
    loads = [pltpu.make_async_copy(h, hv.at[i], h_sem.at[i]) for i, h in enumerate((hist_a, hist_w, hist_g))]
    for copy in moves + loads:
        copy.start()
    count, width = dw.shape[0] // tile, dw.shape[1]
    outs = []
    for n in range(count):
        rows = pl.ds(n * tile, tile)
        y = jnp.dot(At[M - 1, rows], G[M - 1].reshape(-1, width), preferred_element_type=jnp.float32)
        if M > 1:
            y = dw[rows] + y
        held[rows] = y.astype(held.dtype)
        outs.append(pltpu.make_async_copy(held.at[rows], out_w.at[rows], w_sem.at[n]))
        outs[-1].start()
    peaks = top[...]
    for row, out in enumerate((out_ha, out_hw, out_hg)):
        loads[row].wait()
        hn[row] = jnp.concatenate([peaks[row:row + 1, 0:1], hv[row][:, :-1]], axis=1)
        copy = pltpu.make_async_copy(hn.at[row], out, n_sem.at[row])
        copy.start()
        moves.append(copy)
    for copy in moves + outs:
        copy.wait()


def shards(acts_in, weights, cotangent, hist_act, hist_weight, hist_grad):
    S, N, T = lax.axis_size("pipe"), lax.axis_size("dp"), lax.axis_size("tensor")
    M, R, F = acts_in.shape
    chunks = chunks_of(M, R)
    NC, RT = len(chunks), M * R
    FA = T * F // N
    bf, f32 = jnp.bfloat16, jnp.float32
    levels = max(1, T.bit_length() - 1)
    dma = pltpu.SemaphoreType.DMA
    hbm = pl.BlockSpec(memory_space=pltpu.HBM)
    vmem = pl.BlockSpec(memory_space=pltpu.VMEM)
    flat = (RT, F)
    H = hist_act.shape
    hist = jax.ShapeDtypeStruct(H, f32)
    half = max(1, (N + 1) // 2 - 1)
    acts, grads, G, At, dw, top = pl.pallas_call(
        functools.partial(kernel, S, N, T, M, R, F, FA, chunks),
        out_shape=(pltpu.VMEM(flat, bf), pltpu.VMEM(flat, bf),
                   pltpu.VMEM((M, N, R, F), bf), pltpu.VMEM((M, FA, N * R), bf),
                   pltpu.VMEM((FA, F), f32), pltpu.VMEM((8, 128), f32)),
        in_specs=[hbm] * 6,
        out_specs=(vmem,) * 6,
        scratch_shapes=[
            pltpu.VMEM((T, F, F), bf),
            pltpu.VMEM((T, F, F), bf),
            pltpu.VMEM((3,) + H, f32),
            pltpu.VMEM(flat, bf),
            pltpu.VMEM(flat, bf),
            pltpu.VMEM((T,) + flat, bf),
            pltpu.VMEM((max(n for _, _, n in chunks), F), f32),
            pltpu.VMEM(flat, bf),
            pltpu.VMEM((T,) + flat, bf),
            pltpu.VMEM((levels, T) + flat, bf),
            pltpu.VMEM((M, N, R, FA), bf),
            pltpu.VMEM((N * T, 8, 128), f32),
            pltpu.VMEM((16, F), bf),
            pltpu.VMEM((16, F), bf),
            dma((T,)), dma(()), dma((2,)), dma(()), dma(()), dma((NC,)), dma(()), dma((NC, T - 1)),
            dma(()), dma((NC,)), dma(()), dma((NC, T - 1)),
            dma((4,)), dma((NC, N - 1)), dma((2, half, 2)),
            dma(()), dma((M,)), dma(()), dma((M, T - 1)),
            dma(()), dma(()), pltpu.SemaphoreType.REGULAR((max(1, N - 2), 2)),
        ],
        compiler_params=pltpu.CompilerParams(
            collective_id=0, has_side_effects=True, vmem_limit_bytes=40 * 2**20),
    )(*(pltpu.with_memory_space_constraint(v, pltpu.HBM) for v in (
        acts_in.reshape(flat), weights.reshape(T, F, F), cotangent.reshape(flat),
        hist_act, hist_weight, hist_grad)))

    def hold(v):
        return pltpu.with_memory_space_constraint(v, pltpu.VMEM)

    tile = min(256, FA)
    out_acts, out_grads, out_w, ha, hw, hg = pl.pallas_call(
        functools.partial(finish, M, tile),
        out_shape=(jax.ShapeDtypeStruct(flat, bf), jax.ShapeDtypeStruct(flat, bf),
                   jax.ShapeDtypeStruct((FA, F), bf), hist, hist, hist),
        in_specs=[vmem] * 6 + [hbm] * 3,
        out_specs=(hbm,) * 6,
        scratch_shapes=[pltpu.VMEM((FA, F), bf), pltpu.VMEM((3,) + H, f32), pltpu.VMEM((3,) + H, f32),
                        dma((2,)), dma((FA // tile,)), dma((3,)), dma((3,))],
        compiler_params=pltpu.CompilerParams(vmem_limit_bytes=16 * 2**20),
    )(*(hold(v) for v in (acts, grads, G, At, dw, top)), hist_act, hist_weight, hist_grad)
    full = (1, M, R, F)
    return out_acts.reshape(full), out_grads.reshape(full), out_w[None], ha, hw, hg


def solution(mesh):
    placed = (P(None, "dp", "tensor"), P("pipe", None, "tensor"), P(None, "dp", "tensor"),
              P("pipe", None), P("pipe", None), P("pipe", None))
    return jax.shard_map(
        shards, mesh=mesh, in_specs=placed,
        out_specs=(P("pipe", None, "dp", "tensor"), P("pipe", None, "dp", "tensor"),
                   P("pipe", "dp", "tensor"), P("pipe", None), P("pipe", None), P("pipe", None)),
        check_vma=False)
```

time: 85.4 us -> 75.6 us (0.89)
  Pallas kernels: 84.4 us -> 74.5 us
    pallas_call x2, Pallas kernels: 84.4 us -> 74.5 us  [the longest x1 72.3 us: shards(): pl.pallas_call(functools.partial(kernel, S, N, T, M, R, F, FA, chunks), o...]
where the time goes in v1:
time: 75.6 us; the launch traced here: 75.3 us
  Pallas kernels  74.5 us (99%)
  between operations  0.87 us (1%)
    pallas_call x1, Pallas kernels, shards(): pl.pallas_call(functools.partial(kernel, S, N, T, M, R, F, FA, chunks), o...  72.3 us
    pallas_call x1, Pallas kernels, shards(): pl.pallas_call(functools.partial(finish, M, tile), out_shape=(jax.ShapeDt...  2.17 us

profile of v1, /device:TPU:0, one launch (start us, length us, event | category | flops | bytes accessed | tf_op | source)
XLA Modules:
  0.0 75.3 jit_solution(1138103409083373829)
XLA Ops:
  0.6 0.0 copy-start
  0.6 0.0 copy-start.1
  0.7 0.0 copy-start.2
  0.7 72.3 %shard_map.109 = (bf16[256,1024]{1,0:T(8,128)(2,1)S(1)}, bf16[256,1024]{1,0:T(8,128)(2,1)S(1)}, bf16[2,4,128,1024]{3,2,1,0:T(8,128)(2,1)S(1)}, bf16[2,1024,512]{...) custom-call(bf16[256,1024]{1,0:T(8,128)(2,1)} %bitcast.7, bf16[4,1024,1024]{2,1,0:T(8,128)(2,1)} %bitcast.6, ...), custom_call_target="tpu_custom_call" | custom-call | tf_op jit(solution)/shard_map/pallas_call | solution.py:583
  73.0 0.0 copy-done
  73.0 0.0 copy-done.1
  73.0 0.0 copy-done.2
  73.0 2.2 %shard_map.110 = (bf16[256,1024]{1,0:T(8,128)(2,1)}, bf16[256,1024]{1,0:T(8,128)(2,1)}, bf16[1024,1024]{1,0:T(8,128)(2,1)}, f32[1,16]{1,0:T(1,128)}, f32[1,16]{1,0:T(1,128)}, /*index=5*/f32[1,16]{1,0:T(1,128)}) custom-call(bf16[256,1024]{1,0:T(8,128)(2,1)S(1)} %get-tuple-element.18.acts, bf16[256,1024]{1,0:T(8,128)(2,1)S(1)} %get-tuple-element.19.grads, ...), custom_call_target="tpu_custom_call" | custom-call | tf_op jit(solution)/shard_map/pallas_call | solution.py:621
Async XLA Ops:
  0.6 72.3 %copy-start = (f32[1,16]{1,0:T(1,128)S(1)}, f32[1,16]{1,0:T(1,128)}, u32[]{:S(2)}) copy-start(f32[1,16]{1,0:T(1,128)} %hist_a.3) | copy-start | bytes 196
  0.6 72.3 %copy-start.1 = (f32[1,16]{1,0:T(1,128)S(1)}, f32[1,16]{1,0:T(1,128)}, u32[]{:S(2)}) copy-start(f32[1,16]{1,0:T(1,128)} %hist_w.3) | copy-start | bytes 196
  0.7 72.3 %copy-start.2 = (f32[1,16]{1,0:T(1,128)S(1)}, f32[1,16]{1,0:T(1,128)}, u32[]{:S(2)}) copy-start(f32[1,16]{1,0:T(1,128)} %hist_g.3) | copy-start | bytes 196

commit v2 on v1

--- a/solution.py
+++ b/solution.py
@@ -8,7 +8,8 @@
 from jax.sharding import PartitionSpec as P
 
 MESH = pl.DeviceIdType.MESH
-FIRST, LATER = (4, 4, 2), (2, 2)
+PARTS = 8
+FIRST, LATER = (2, 3, 3), (4, 4)
 
 
 def strides_below(index, count):
@@ -29,21 +30,23 @@
     for m in range(M):
         start = 0
         for part in FIRST if m == 0 else LATER:
-            found.append((m, start, R // part))
-            start += R // part
+            found.append((m, start, R * part // PARTS))
+            start += R * part // PARTS
     return found
 
 
 def kernel(S, N, T, M, R, F, FA, chunks,
            acts, weights, cot, hist_a, hist_w, hist_g,
            xout, gout, G, At, dw, out_top,
-           w, wt, hv, cv, xin, xg, acc, gin, part, rs, A, pk, amax, gmax,
+           w, wt, hv, cv, xin, xg, acc, gin, part, rs, A, pk, amax, gmax, gd, gh,
            w_sem, h_sem, in_sem, c_sem, x_ss, x_rs, ag_ss, ag_rs, g_ss, g_rs, rd_ss, rd_rs,
-           G_ss, G_rs, Gr_ss, A_ss, A_rs, B_ss, B_rs, p_ss, p_rs, hello):
+           G_ss, G_rs, Gr_ss, Gm_ss, A_ss, A_rs, B_ss, B_rs, p_ss, p_rs, hello, ready,
+           gd_ss, gd_rs):
     s, d, t = lax.axis_index("pipe"), lax.axis_index("dp"), lax.axis_index("tensor")
     last = S - 1
     bf, f32 = jnp.bfloat16, jnp.float32
     NC = len(chunks)
+    top = T // 2
     stages = []
     st = 1
     while st < T:
@@ -145,11 +148,14 @@
     up = jnp.minimum(s + 1, last)
     down = jnp.maximum(s - 1, 0)
 
+    def gd_copy(c):
+        return remote(part.at[top, rows_at(c)], gd.at[rows_at(c)], gd_ss, gd_rs.at[c], pipe=down, tensor=t ^ top)
+
     def x_copy(c):
         return remote(xout.at[rows_at(c)], xin.at[rows_at(c)], x_ss, x_rs.at[c], pipe=up)
 
     def g_copy(c):
-        return remote(gout.at[rows_at(c)], gin.at[rows_at(c)], g_ss, g_rs.at[c], pipe=down)
+        return remote(gh.at[rows_at(c)], gin.at[rows_at(c)], g_ss, g_rs.at[c], pipe=down)
 
     def ag_copy(c, j, st):
         i = j ^ st
@@ -168,15 +174,28 @@
     def inside(at):
         return (at >= 0) & (at < N)
 
-    def own_sends(act):
-        for i, step in enumerate((1, -1, 2, -2)):
+    def own_sends(act, mix=False):
+        for i, step in enumerate((2, -2, 1, -1)):
             if abs(step) < N:
-                @pl.when(inside(d + step))
+                here = inside(d + step)
+                if mix and abs(step) == 2:
+                    here = here & inside(d + step + step // 2)
+
+                @pl.when(here)
                 def _(i=i, to=d + step):
                     act(to, G_ss.at[i])
 
-    def relays(wait, act):
+    def near_end(way):
+        return inside(d - way) & inside(d + way) & ~inside(d + 2 * way)
+
+    def relays(wait, act, mix=False):
         for i, way in enumerate((1, -1)):
+            if mix:
+                @pl.when(near_end(way))
+                def _(i=i, way=way):
+                    wait(d - way)
+                    act(d - way, d + way, Gm_ss.at[i])
+
             for m in range(1, (N + 1) // 2):
                 origin = d - way * 2 * m
 
@@ -195,24 +214,25 @@
         start = lax.rem(r, ratio) * FA
         return t ^ lax.div(r, ratio), pl.ds(pl.multiple_of(start, FA), FA)
 
-    piece = R // T
-
-    def rows_of(owner):
+    piece = FA // T
+
+    def cols_of(owner):
         return pl.ds(pl.multiple_of(owner * piece, piece), piece)
 
-    def A_copy(m, k):
-        owner, cols = in_block(d ^ k)
-        src = pl.ds(pl.multiple_of(m * R + t * piece, piece), piece)
-        return remote(xg.at[owner, src, cols], A.at[m, k, rows_of(t)],
-                      A_ss, A_rs.at[m], dp=d ^ k)
+    def A_copy(c, k):
+        m, start, n = chunks[c]
+        r = d ^ k
+        cols = pl.ds(pl.multiple_of(lax.rem(r, ratio) * FA + t * piece, piece), piece)
+        return remote(xg.at[t ^ lax.div(r, ratio), rows_at(c), cols], A.at[m, k, pl.ds(start, n), cols_of(t)],
+                      A_ss, A_rs.at[m], dp=r)
 
     def B_copy(m, j, st):
         i = j ^ st
-        there = A.at[m, pl.ds(1, N - 1), rows_of(t ^ j)]
+        there = A.at[m, pl.ds(1, N - 1), :, cols_of(t ^ j)]
         return remote(there, there, B_ss, B_rs.at[m, i - 1], tensor=t ^ st)
 
     def B_arrival(m, i):
-        there = A.at[m, pl.ds(1, N - 1), rows_of(t ^ i)]
+        there = A.at[m, pl.ds(1, N - 1), :, cols_of(t ^ i)]
         return remote(there, there, B_ss, B_rs.at[m, i - 1], tensor=t ^ low(i))
 
     def rd_copy(c, j, level):
@@ -253,8 +273,8 @@
             peak = lax.fori_loop(0, F // 128, body, peak)
         return jnp.max(peak.astype(f32), keepdims=True).reshape(1, 1)
 
-    def turn_weights():
-        for b in range(T):
+    def turn_weights(first, end):
+        for b in range(first, end):
             def body(i, _, b=b):
                 rows = pl.ds(pl.multiple_of(i * 128, 128), 128)
                 wt[b, :, rows] = w[b, rows].T
@@ -288,15 +308,19 @@
             else:
                 xout[rows] = (acc[:n] + term(j) + xin[rows].astype(f32)).astype(bf)
 
+        if c == 0 and top:
+            pl.semaphore_wait(ready, 1)
+
         @pl.when(s < last)
         def _():
             x_copy(c).start()
 
-    def send_A(m):
+    def send_A(c):
+        m, start, n = chunks[c]
         for k in range(1, N):
-            A_copy(m, k).start()
+            A_copy(c, k).start()
         owner, cols = in_block(d)
-        A[m, 0] = xg[owner, pl.ds(m * R, R), cols]
+        A[m, 0, pl.ds(start, n)] = xg[owner, rows_at(c), cols]
 
     def bwd(c, is_last):
         m, start, n = chunks[c]
@@ -305,10 +329,17 @@
             gin[rows] = (cv[rows].astype(f32) * xout[rows].astype(f32)).astype(bf)
         else:
             g_copy(c).wait_recv()
+            if top:
+                gd_copy(c).wait_recv()
+                gin[rows] = (gin[rows].astype(f32) + gd[rows].astype(f32)).astype(bf)
         g = gin[rows]
         G[m, 0, pl.ds(start, n)] = clip(g, lim_g)
-        own_sends(lambda to, ss: G_copy(c, d, to, ss).start())
-        gmax[...] = jnp.maximum(gmax[...], fold(g))
+        if c == NC - 1:
+            gmax[...] = jnp.maximum(gmax[...], fold(g))
+            send_peaks()
+        send_G(c, is_last)
+        if c < NC - 1:
+            gmax[...] = jnp.maximum(gmax[...], fold(g))
 
         def settle(j):
             level = 0
@@ -317,44 +348,75 @@
                 part[j, rows] = (part[j, rows].astype(f32) + rs[level, j, rows].astype(f32)).astype(bf)
                 level += 1
             rd_copy(c, j, level).start()
-
-        for j in reversed(range(T)):
-            y = jnp.dot(G[m, 0, pl.ds(start, n)], wt[t ^ j], preferred_element_type=f32)
-            part[j, rows] = y.astype(bf)
-            if j & 1:
-                rd_copy(c, j, 0).start()
-                if j + 1 < T:
-                    settle(j + 1)
+            if j == top:
+                @pl.when(s > 0)
+                def _():
+                    gd_copy(c).start()
+
+        def term(j):
+            return jnp.dot(G[m, 0, pl.ds(start, n)], wt[t ^ j], preferred_element_type=f32).astype(bf)
+
+        for j in reversed(range(1, T, 2)):
+            y, z = term(j), term(j - 1)
+            part[j, rows] = y
+            part[j - 1, rows] = z
+            rd_copy(c, j, 0).start()
+            if j + 1 < T:
+                settle(j + 1)
+        if T == 1:
+            part[0, rows] = term(0)
+
+    def pass_on(c):
+        rows = rows_at(c)
+
+        @pl.when(s > 0)
+        def _():
+            total = gin[rows].astype(f32) + part[0, rows].astype(f32)
+            for level in range(len(stages) - 1):
+                rd_copy(c, stages[level], level).wait_recv()
+                total = total + rs[level, 0, rows].astype(f32)
+            gh[rows] = total.astype(bf)
+            g_copy(c).start()
+
+    def mixed(c, is_last):
+        return is_last and M > 1 and 0 < c and chunks[c][0] == 0
+
+    def send_G(c, is_last):
+        own_sends(lambda to, ss: G_copy(c, d, to, ss).start(), mixed(c, is_last))
 
     def finb(c):
         rows = rows_at(c)
         total = gin[rows].astype(f32) + part[0, rows].astype(f32)
         for level in range(len(stages)):
-            rd_copy(c, stages[level], level).wait_recv()
+            if level < len(stages) - 1:
+                @pl.when(s == 0)
+                def _(level=level):
+                    rd_copy(c, stages[level], level).wait_recv()
+            else:
+                rd_copy(c, stages[level], level).wait_recv()
             total = total + rs[level, 0, rows].astype(f32)
         gout[rows] = total.astype(bf)
 
-        @pl.when(s > 0)
-        def _():
-            g_copy(c).start()
-
-    def relay_G(c):
-        relays(lambda origin: G_wait(c, origin), lambda origin, to, ss: G_copy(c, origin, to, ss).start())
-
-    def arrive_G(c):
+    def relay_G(c, is_last=False):
+        relays(lambda origin: G_wait(c, origin), lambda origin, to, ss: G_copy(c, origin, to, ss).start(),
+               mixed(c, is_last))
+
+    def arrive_G(c, is_last=False):
         for step in range(1, N):
             for way in (1, -1):
                 origin = d - way * step
                 here = inside(origin)
                 if step % 2 == 0:
                     here = here & ~inside(d + way)
+                elif step == 1 and mixed(c, is_last):
+                    here = here & ~near_end(way)
 
                 @pl.when(here)
                 def _(origin=origin):
                     G_wait(c, origin)
 
     def relay_A(m):
-        there = A.at[m, pl.ds(1, N - 1), rows_of(t)]
+        there = A.at[m, pl.ds(1, N - 1), :, cols_of(t)]
         remote(there, there, A_ss, A_rs.at[m], dp=d ^ 1).wait_recv()
         for st in strides_below(0, T):
             B_copy(m, 0, st).start()
@@ -379,8 +441,10 @@
             lax.fori_loop(0, FA // 128, body, 0)
 
     def update(m):
+        tile = min(256, FA)
+
         def body(n, _):
-            rows = pl.ds(pl.multiple_of(n * 128, 128), 128)
+            rows = pl.ds(pl.multiple_of(n * tile, tile), tile)
             y = jnp.dot(At[m, rows], G[m].reshape(N * R, F), preferred_element_type=f32)
             if m == 0:
                 dw[rows] = y
@@ -388,7 +452,7 @@
                 dw[rows] += y
             return 0
 
-        lax.fori_loop(0, FA // 128, body, 0)
+        lax.fori_loop(0, FA // tile, body, 0)
 
     def peers():
         return [(k, j) for k in range(N) for j in range(T) if k or j]
@@ -415,6 +479,8 @@
 
     enter()
     greet(0)
+    if top:
+        signal(ready, tensor=t ^ top)
 
     @pl.when(s == 0)
     def _():
@@ -425,45 +491,45 @@
 
     @pl.when(s > 0)
     def _():
-        turn_weights()
-        meet(0, N - 2)
+        meet(0, 1)
+        turn_weights(0, T)
         prep(0)
         prep(1)
-
-    def arrive(m):
+        meet(1, N - 2)
+
+    def arrive(m, is_last=False):
         for c in range(NC):
             if chunks[c][0] == m:
-                arrive_G(c)
+                arrive_G(c, is_last)
 
     @pl.when(s == last)
     def _():
         cot_load.wait()
         for c in range(NC):
             fwd(c)
-            if c in ends:
-                send_A(ends.index(c))
+            send_A(c)
             bwd(c, True)
-            if c == NC - 1:
-                send_peaks()
             if c + 2 < NC:
                 prep(c + 2)
-            if c:
-                finb(c - 1)
+            if c == 1:
+                relay_G(0, True)
+            if c >= 3:
+                relay_G(c - 2, True)
+            pass_on(c)
             if c >= 2:
-                relay_G(c - 2)
-        finb(NC - 1)
-        for m in range(M - 1):
+                finb(c - 2)
+        for c in range(max(0, NC - 2), NC):
+            finb(c)
+        relay_G(NC - 2, True)
+        for m in range(M):
             relay_A(m)
-        relay_G(NC - 2)
-        relay_A(M - 1)
-        for m in range(M - 1):
+            if m:
+                arrive(m - 1, True)
+                update(m - 1)
             relay_B(m)
+            if m == M - 1:
+                relay_G(NC - 1, True)
             turn_A(m)
-            arrive(m)
-            update(m)
-        relay_B(M - 1)
-        relay_G(NC - 1)
-        turn_A(M - 1)
 
     @pl.when(s < last)
     def _():
@@ -475,34 +541,37 @@
                 @pl.when(s == 0)
                 def _(c=c):
                     meet(max(0, N - 3) * c, N - 3 + c)
-            if c in ends:
-                send_A(ends.index(c))
-
-        @pl.when(s == 0)
-        def _():
-            turn_weights()
+            if c:
+                for b in range(0 if c == 1 else c, c + 1):
+                    send_A(b)
+
+                @pl.when(s == 0)
+                def _(c=c):
+                    turn_weights(T * c // NC if c > 1 else 0, T * (c + 1) // NC)
 
         relay_A(0)
         for c in range(NC):
+            if c >= 2:
+                relay_G(c - 1)
             bwd(c, False)
-            if c == NC - 1:
-                send_peaks()
-            if c:
-                finb(c - 1)
-            if c < M - 1:
-                relay_A(c + 1)
-            if 1 <= c <= M:
-                relay_B(c - 1)
+            pass_on(c)
+            if c == 1:
+                relay_G(0)
+            if 1 <= c < M:
+                relay_A(c)
             if c >= 2:
-                relay_G(c - 2)
-            if 2 <= c < M + 2:
-                turn_A(c - 2)
-        relay_G(NC - 2)
+                finb(c - 2)
+                if c - 2 < M:
+                    relay_B(c - 2)
+            if 3 <= c < M + 3:
+                turn_A(c - 3)
+        for c in range(max(0, NC - 2), NC - 1):
+            finb(c)
+        relay_G(NC - 1)
         finb(NC - 1)
         for m in range(M - 1):
             arrive(m)
             update(m)
-        relay_G(NC - 1)
 
     arrive(M - 1)
 
@@ -515,10 +584,33 @@
         remote(ref, ref, sem, p_rs, dp=d ^ 1).wait_send()
 
     def finalwait():
-        most = pl.ds(0, T - 1)
-        sent(xg.at[most], ag_ss)
-        sent(part.at[most], rd_ss)
-        own_sends(lambda to, ss: sent(gin, ss))
+        if top:
+            sent(xg.at[pl.ds(0, T - 1)], ag_ss)
+            sent(part.at[pl.ds(0, T - 1)], rd_ss)
+
+            @pl.when(s > 0)
+            def _():
+                sent(gin, gd_ss)
+
+        def own_sent(to, ss):
+            sent(gin, ss)
+
+        @pl.when(s < last)
+        def _():
+            own_sends(own_sent)
+
+        @pl.when(s == last)
+        def _():
+            if M > 1:
+                own_sends(lambda to, ss: sent(gin.at[pl.ds(0, R - first)], ss), True)
+                own_sends(lambda to, ss: sent(gin.at[pl.ds(R - first, (M - 1) * R + first)], ss))
+                for i, way in enumerate((1, -1)):
+                    @pl.when(near_end(way))
+                    def _(i=i):
+                        sent(gin.at[pl.ds(0, R - first)], Gm_ss.at[i])
+            else:
+                own_sends(own_sent)
+
         relays(lambda origin: None, lambda origin, to, ss: sent(gin, ss))
 
         @pl.when(s < last)
@@ -529,8 +621,8 @@
         def _():
             sent(gin, g_ss)
 
-        sent(A.at[:, pl.ds(1, N - 1), rows_of(t)], A_ss)
-        sent(A.at[:, pl.ds(1, N - 1), pl.ds(0, (T - 1) * piece)], B_ss)
+        sent(A.at[:, pl.ds(1, N - 1), :, cols_of(t)], A_ss)
+        sent(A.at[:, pl.ds(1, N - 1), :, pl.ds(0, (T - 1) * piece)], B_ss)
         sent(pk.at[pl.ds(1, N * T - 1)], p_ss)
 
     peakwait()
@@ -602,11 +694,14 @@
             pltpu.VMEM((N * T, 8, 128), f32),
             pltpu.VMEM((16, F), bf),
             pltpu.VMEM((16, F), bf),
+            pltpu.VMEM(flat, bf),
+            pltpu.VMEM(flat, bf),
             dma((T,)), dma(()), dma((2,)), dma(()), dma(()), dma((NC,)), dma(()), dma((NC, T - 1)),
             dma(()), dma((NC,)), dma(()), dma((NC, T - 1)),
-            dma((4,)), dma((NC, N - 1)), dma((2, half, 2)),
+            dma((4,)), dma((NC, N - 1)), dma((2, half, 2)), dma((2,)),
             dma(()), dma((M,)), dma(()), dma((M, T - 1)),
             dma(()), dma(()), pltpu.SemaphoreType.REGULAR((max(1, N - 2), 2)),
+            pltpu.SemaphoreType.REGULAR, dma(()), dma((NC,)),
         ],
         compiler_params=pltpu.CompilerParams(
             collective_id=0, has_side_effects=True, vmem_limit_bytes=40 * 2**20),

time: 75.6 us -> 68.9 us (0.911)
  Pallas kernels: 74.5 us -> 67.6 us
    pallas_call x1, Pallas kernels: 72.3 us -> 65.4 us  [shards(): pl.pallas_call(functools.partial(kernel, S, N, T, M, R, F, FA, chunks), o...]
where the time goes in v2:
time: 68.9 us; the launch traced here: 68.4 us
  Pallas kernels  67.6 us (98%)
  between operations  0.85 us (1%)
    pallas_call x1, Pallas kernels, shards(): pl.pallas_call(functools.partial(kernel, S, N, T, M, R, F, FA, chunks), o...  65.4 us
    pallas_call x1, Pallas kernels, shards(): pl.pallas_call(functools.partial(finish, M, tile), out_shape=(jax.ShapeDt...  2.17 us

profile of v2, /device:TPU:0, one launch (start us, length us, event | category | flops | bytes accessed | tf_op | source)
XLA Modules:
  0.0 68.4 jit_solution(3648792451695399054)
XLA Ops:
  0.6 0.0 copy-start
  0.6 0.0 copy-start.1
  0.7 0.0 copy-start.2
  0.7 65.4 %shard_map.109 = (bf16[256,1024]{1,0:T(8,128)(2,1)S(1)}, bf16[256,1024]{1,0:T(8,128)(2,1)S(1)}, bf16[2,4,128,1024]{3,2,1,0:T(8,128)(2,1)S(1)}, bf16[2,1024,512]{...) custom-call(bf16[256,1024]{1,0:T(8,128)(2,1)} %bitcast.7, bf16[4,1024,1024]{2,1,0:T(8,128)(2,1)} %bitcast.6, ...), custom_call_target="tpu_custom_call" | custom-call | tf_op jit(solution)/shard_map/pallas_call | solution.py:675
  66.1 0.0 copy-done
  66.1 0.0 copy-done.1
  66.1 0.0 copy-done.2
  66.1 2.2 %shard_map.110 = (bf16[256,1024]{1,0:T(8,128)(2,1)}, bf16[256,1024]{1,0:T(8,128)(2,1)}, bf16[1024,1024]{1,0:T(8,128)(2,1)}, f32[1,16]{1,0:T(1,128)}, f32[1,16]{1,0:T(1,128)}, /*index=5*/f32[1,16]{1,0:T(1,128)}) custom-call(bf16[256,1024]{1,0:T(8,128)(2,1)S(1)} %get-tuple-element.18.acts, bf16[256,1024]{1,0:T(8,128)(2,1)S(1)} %get-tuple-element.19.grads, ...), custom_call_target="tpu_custom_call" | custom-call | tf_op jit(solution)/shard_map/pallas_call | solution.py:716
Async XLA Ops:
  0.6 65.4 %copy-start = (f32[1,16]{1,0:T(1,128)S(1)}, f32[1,16]{1,0:T(1,128)}, u32[]{:S(2)}) copy-start(f32[1,16]{1,0:T(1,128)} %hist_a.3) | copy-start | bytes 196
  0.6 65.4 %copy-start.1 = (f32[1,16]{1,0:T(1,128)S(1)}, f32[1,16]{1,0:T(1,128)}, u32[]{:S(2)}) copy-start(f32[1,16]{1,0:T(1,128)} %hist_w.3) | copy-start | bytes 196
  0.7 65.4 %copy-start.2 = (f32[1,16]{1,0:T(1,128)S(1)}, f32[1,16]{1,0:T(1,128)}, u32[]{:S(2)}) copy-start(f32[1,16]{1,0:T(1,128)} %hist_g.3) | copy-start | bytes 196

commit v3 on v2

--- a/solution.py
+++ b/solution.py
@@ -35,9 +35,13 @@
     return found
 
 
+def units_of(M, R):
+    return [(0, 0, R)] + [chunk for chunk in chunks_of(M, R) if chunk[0]]
+
+
 def kernel(S, N, T, M, R, F, FA, chunks,
            acts, weights, cot, hist_a, hist_w, hist_g,
-           xout, gout, G, At, dw, out_top,
+           xout, gout, G, At, dw, new_hist,
            w, wt, hv, cv, xin, xg, acc, gin, part, rs, A, pk, amax, gmax, gd, gh,
            w_sem, h_sem, in_sem, c_sem, x_ss, x_rs, ag_ss, ag_rs, g_ss, g_rs, rd_ss, rd_rs,
            G_ss, G_rs, Gr_ss, Gm_ss, A_ss, A_rs, B_ss, B_rs, p_ss, p_rs, hello, ready,
@@ -46,6 +50,8 @@
     last = S - 1
     bf, f32 = jnp.bfloat16, jnp.float32
     NC = len(chunks)
+    units = units_of(M, R)
+    U = len(units)
     top = T // 2
     stages = []
     st = 1
@@ -219,21 +225,28 @@
     def cols_of(owner):
         return pl.ds(pl.multiple_of(owner * piece, piece), piece)
 
+    def unit_of(c):
+        return 0 if chunks[c][0] == 0 else units.index(chunks[c])
+
+    def block(u, which, cols):
+        m, start, n = units[u]
+        return A.at[m, which, pl.ds(start, n), cols]
+
     def A_copy(c, k):
         m, start, n = chunks[c]
         r = d ^ k
         cols = pl.ds(pl.multiple_of(lax.rem(r, ratio) * FA + t * piece, piece), piece)
         return remote(xg.at[t ^ lax.div(r, ratio), rows_at(c), cols], A.at[m, k, pl.ds(start, n), cols_of(t)],
-                      A_ss, A_rs.at[m], dp=r)
-
-    def B_copy(m, j, st):
+                      A_ss, A_rs.at[unit_of(c)], dp=r)
+
+    def B_copy(u, j, st):
         i = j ^ st
-        there = A.at[m, pl.ds(1, N - 1), :, cols_of(t ^ j)]
-        return remote(there, there, B_ss, B_rs.at[m, i - 1], tensor=t ^ st)
-
-    def B_arrival(m, i):
-        there = A.at[m, pl.ds(1, N - 1), :, cols_of(t ^ i)]
-        return remote(there, there, B_ss, B_rs.at[m, i - 1], tensor=t ^ low(i))
+        there = block(u, pl.ds(1, N - 1), cols_of(t ^ j))
+        return remote(there, there, B_ss, B_rs.at[u, i - 1], tensor=t ^ st)
+
+    def B_arrival(u, i):
+        there = block(u, pl.ds(1, N - 1), cols_of(t ^ i))
+        return remote(there, there, B_ss, B_rs.at[u, i - 1], tensor=t ^ low(i))
 
     def rd_copy(c, j, level):
         st = stages[level]
@@ -282,7 +295,7 @@
 
             lax.fori_loop(0, F // 128, body, 0)
 
-    def fwd(c):
+    def fwd(c, between=None):
         rows = rows_at(c)
         n = chunks[c][2]
 
@@ -303,6 +316,8 @@
                     xout[rows] = (y + xin[rows].astype(f32)).astype(bf)
                 else:
                     acc[:n] = y
+                    if between:
+                        between()
             elif j < T - 1:
                 acc[:n] += term(j)
             else:
@@ -415,38 +430,43 @@
                 def _(origin=origin):
                     G_wait(c, origin)
 
-    def relay_A(m):
-        there = A.at[m, pl.ds(1, N - 1), :, cols_of(t)]
-        remote(there, there, A_ss, A_rs.at[m], dp=d ^ 1).wait_recv()
+    def relay_A(u):
+        there = block(u, pl.ds(1, N - 1), cols_of(t))
+        remote(there, there, A_ss, A_rs.at[u], dp=d ^ 1).wait_recv()
         for st in strides_below(0, T):
-            B_copy(m, 0, st).start()
-
-    def relay_B(m):
+            B_copy(u, 0, st).start()
+
+    def relay_B(u):
         for j in range(1, T):
             if strides_below(j, T):
-                B_arrival(m, j).wait_recv()
+                B_arrival(u, j).wait_recv()
                 for st in strides_below(j, T):
-                    B_copy(m, j, st).start()
-
-    def turn_A(m):
+                    B_copy(u, j, st).start()
+
+    def turn_A(u):
+        m, start, n = units[u]
+        group = max(1, 128 // n)
         for j in range(1, T):
             if not strides_below(j, T):
-                B_arrival(m, j).wait_recv()
-        for k in range(N):
+                B_arrival(u, j).wait_recv()
+        for k in range(0, N, group):
             def body(i, _, k=k):
                 cols = pl.ds(pl.multiple_of(i * 128, 128), 128)
-                At[m, cols, pl.ds(k * R, R)] = A[m, k, :, cols].T
+                v = A[m, pl.ds(k, group), pl.ds(start, n), cols].reshape(group * n, 128)
+                At[cols, pl.ds(N * (m * R + start) + k * n, group * n)] = v.T
                 return 0
 
             lax.fori_loop(0, FA // 128, body, 0)
 
-    def update(m):
+    def update(u):
+        m, start, n = units[u]
         tile = min(256, FA)
 
-        def body(n, _):
-            rows = pl.ds(pl.multiple_of(n * tile, tile), tile)
-            y = jnp.dot(At[m, rows], G[m].reshape(N * R, F), preferred_element_type=f32)
-            if m == 0:
+        def body(i, _):
+            rows = pl.ds(pl.multiple_of(i * tile, tile), tile)
+            y = jnp.dot(At[rows, pl.ds(N * (m * R + start), N * n)], G[m, :, pl.ds(start, n)].reshape(N * n, F),
+                        preferred_element_type=f32)
+            if u == 0:
                 dw[rows] = y
             else:
                 dw[rows] += y
@@ -494,19 +514,18 @@
         meet(0, 1)
         turn_weights(0, T)
         prep(0)
-        prep(1)
         meet(1, N - 2)
 
-    def arrive(m, is_last=False):
+    def arrive(u, is_last=False):
         for c in range(NC):
-            if chunks[c][0] == m:
+            if unit_of(c) == u:
                 arrive_G(c, is_last)
 
     @pl.when(s == last)
     def _():
         cot_load.wait()
         for c in range(NC):
-            fwd(c)
+            fwd(c, functools.partial(pass_on, c - 1) if c else functools.partial(prep, 1))
             send_A(c)
             bwd(c, True)
             if c + 2 < NC:
@@ -515,24 +534,38 @@
                 relay_G(0, True)
             if c >= 3:
                 relay_G(c - 2, True)
-            pass_on(c)
             if c >= 2:
                 finb(c - 2)
+        pass_on(NC - 1)
         for c in range(max(0, NC - 2), NC):
             finb(c)
         relay_G(NC - 2, True)
-        for m in range(M):
-            relay_A(m)
-            if m:
-                arrive(m - 1, True)
-                update(m - 1)
-            relay_B(m)
-            if m == M - 1:
-                relay_G(NC - 1, True)
-            turn_A(m)
+        for u in range(U):
+            if 1 < u:
+                turn_A(u - 2)
+                relay_B(u - 1)
+            relay_A(u)
+            if u == 1:
+                relay_B(0)
+        if U > 1:
+            turn_A(U - 2)
+        for u in range(min(1, U - 1)):
+            arrive(u, True)
+            update(u)
+        relay_B(U - 1)
+        relay_G(NC - 1, True)
+        turn_A(U - 1)
+        for u in range(1, U - 1):
+            arrive(u, True)
+            update(u)
 
     @pl.when(s < last)
     def _():
+        @pl.when(s > 0)
+        def _():
+            prep(1)
+
+        spread = [0, 0] + [min(T, max(1, T - NC + c)) for c in range(2, NC)] + [T]
         for c in range(NC):
             fwd(c)
             if c + 2 < NC:
@@ -547,38 +580,38 @@
 
                 @pl.when(s == 0)
                 def _(c=c):
-                    turn_weights(T * c // NC if c > 1 else 0, T * (c + 1) // NC)
-
-        relay_A(0)
-        for c in range(NC):
-            if c >= 2:
+                    turn_weights(spread[c], spread[c + 1])
+
+        for c in range(NC + 3):
+            if c == 0:
+                relay_A(0)
+            if c == NC:
+                relay_G(NC - 1)
+            if 1 <= c < NC:
                 relay_G(c - 1)
-            bwd(c, False)
-            pass_on(c)
-            if c == 1:
-                relay_G(0)
-            if 1 <= c < M:
+            if c < NC:
+                bwd(c, False)
+                pass_on(c)
+            if 1 <= c < U:
                 relay_A(c)
-            if c >= 2:
+            if 2 <= c < NC + 2:
                 finb(c - 2)
-                if c - 2 < M:
-                    relay_B(c - 2)
-            if 3 <= c < M + 3:
+            if 2 <= c < U + 2:
+                relay_B(c - 2)
+            if 3 <= c < U + 3:
                 turn_A(c - 3)
-        for c in range(max(0, NC - 2), NC - 1):
-            finb(c)
-        relay_G(NC - 1)
-        finb(NC - 1)
-        for m in range(M - 1):
-            arrive(m)
-            update(m)
-
-    arrive(M - 1)
+        for u in range(U - 1):
+            arrive(u)
+            update(u)
+
+    arrive(U - 1)
 
     def peakwait():
         there = pk.at[pl.ds(1, N * T - 1)]
         remote(there, there, p_ss, p_rs, dp=d ^ 1).wait_recv()
-        out_top[...] = jnp.max(pk[...], axis=0)
+        peaks = jnp.max(pk[...], axis=0)
+        for i in range(3):
+            new_hist[i] = jnp.concatenate([peaks[i:i + 1, 0:1], hv[i][:, :-1]], axis=1)
 
     def sent(ref, sem):
         remote(ref, ref, sem, p_rs, dp=d ^ 1).wait_send()
@@ -629,31 +662,25 @@
     finalwait()
 
 
-def finish(M, tile, acts, grads, G, At, dw, top, hist_a, hist_w, hist_g,
-           out_acts, out_grads, out_w, out_ha, out_hw, out_hg, held, hv, hn, sem, w_sem, h_sem, n_sem):
+def finish(unit, lanes, tile, acts, grads, G, At, dw, new_hist,
+           out_acts, out_grads, out_w, out_ha, out_hw, out_hg, held, sem, w_sem, h_sem):
+    m, start, n = unit
     moves = [pltpu.make_async_copy(acts, out_acts, sem.at[0]),
              pltpu.make_async_copy(grads, out_grads, sem.at[1])]
-    loads = [pltpu.make_async_copy(h, hv.at[i], h_sem.at[i]) for i, h in enumerate((hist_a, hist_w, hist_g))]
-    for copy in moves + loads:
+    for i, out in enumerate((out_ha, out_hw, out_hg)):
+        moves.append(pltpu.make_async_copy(new_hist.at[i], out, h_sem.at[i]))
+    for copy in moves:
         copy.start()
     count, width = dw.shape[0] // tile, dw.shape[1]
-    outs = []
-    for n in range(count):
-        rows = pl.ds(n * tile, tile)
-        y = jnp.dot(At[M - 1, rows], G[M - 1].reshape(-1, width), preferred_element_type=jnp.float32)
-        if M > 1:
+    for i in range(count):
+        rows = pl.ds(i * tile, tile)
+        y = jnp.dot(At[rows, lanes], G[m, :, pl.ds(start, n)].reshape(-1, width), preferred_element_type=jnp.float32)
+        if m:
             y = dw[rows] + y
         held[rows] = y.astype(held.dtype)
-        outs.append(pltpu.make_async_copy(held.at[rows], out_w.at[rows], w_sem.at[n]))
-        outs[-1].start()
-    peaks = top[...]
-    for row, out in enumerate((out_ha, out_hw, out_hg)):
-        loads[row].wait()
-        hn[row] = jnp.concatenate([peaks[row:row + 1, 0:1], hv[row][:, :-1]], axis=1)
-        copy = pltpu.make_async_copy(hn.at[row], out, n_sem.at[row])
-        copy.start()
-        moves.append(copy)
-    for copy in moves + outs:
+        moves.append(pltpu.make_async_copy(held.at[rows], out_w.at[rows], w_sem.at[i]))
+        moves[-1].start()
+    for copy in moves:
         copy.wait()
 
 
@@ -672,11 +699,13 @@
     H = hist_act.shape
     hist = jax.ShapeDtypeStruct(H, f32)
     half = max(1, (N + 1) // 2 - 1)
-    acts, grads, G, At, dw, top = pl.pallas_call(
+    units = units_of(M, R)
+    unit = units[-1]
+    acts, grads, G, At, dw, new_hist = pl.pallas_call(
         functools.partial(kernel, S, N, T, M, R, F, FA, chunks),
         out_shape=(pltpu.VMEM(flat, bf), pltpu.VMEM(flat, bf),
-                   pltpu.VMEM((M, N, R, F), bf), pltpu.VMEM((M, FA, N * R), bf),
-                   pltpu.VMEM((FA, F), f32), pltpu.VMEM((8, 128), f32)),
+                   pltpu.VMEM((M, N, R, F), bf), pltpu.VMEM((FA, N * RT), bf),
+                   pltpu.VMEM((FA, F), f32), pltpu.VMEM((3,) + H, f32)),
         in_specs=[hbm] * 6,
         out_specs=(vmem,) * 6,
         scratch_shapes=[
@@ -699,7 +728,7 @@
             dma((T,)), dma(()), dma((2,)), dma(()), dma(()), dma((NC,)), dma(()), dma((NC, T - 1)),
             dma(()), dma((NC,)), dma(()), dma((NC, T - 1)),
             dma((4,)), dma((NC, N - 1)), dma((2, half, 2)), dma((2,)),
-            dma(()), dma((M,)), dma(()), dma((M, T - 1)),
+            dma(()), dma((len(units),)), dma(()), dma((len(units), T - 1)),
             dma(()), dma(()), pltpu.SemaphoreType.REGULAR((max(1, N - 2), 2)),
             pltpu.SemaphoreType.REGULAR, dma(()), dma((NC,)),
         ],
@@ -714,15 +743,14 @@
 
     tile = min(256, FA)
     out_acts, out_grads, out_w, ha, hw, hg = pl.pallas_call(
-        functools.partial(finish, M, tile),
+        functools.partial(finish, unit, pl.ds(N * (RT - unit[2]), N * unit[2]), tile),
         out_shape=(jax.ShapeDtypeStruct(flat, bf), jax.ShapeDtypeStruct(flat, bf),
                    jax.ShapeDtypeStruct((FA, F), bf), hist, hist, hist),
-        in_specs=[vmem] * 6 + [hbm] * 3,
+        in_specs=[vmem] * 6,
         out_specs=(hbm,) * 6,
-        scratch_shapes=[pltpu.VMEM((FA, F), bf), pltpu.VMEM((3,) + H, f32), pltpu.VMEM((3,) + H, f32),
-                        dma((2,)), dma((FA // tile,)), dma((3,)), dma((3,))],
+        scratch_shapes=[pltpu.VMEM((FA, F), bf), dma((2,)), dma((FA // tile,)), dma((3,))],
         compiler_params=pltpu.CompilerParams(vmem_limit_bytes=16 * 2**20),
-    )(*(hold(v) for v in (acts, grads, G, At, dw, top)), hist_act, hist_weight, hist_grad)
+    )(*(hold(v) for v in (acts, grads, G, At, dw, new_hist)))
     full = (1, M, R, F)
     return out_acts.reshape(full), out_grads.reshape(full), out_w[None], ha, hw, hg
 

time: 68.9 us -> 67.7 us (0.983)
  Pallas kernels: 67.6 us -> 66.3 us
    pallas_call x1, Pallas kernels: 65.4 us -> 64.3 us  [shards(): pl.pallas_call(functools.partial(kernel, S, N, T, M, R, F, FA, chunks), o...]
where the time goes in v3:
time: 67.7 us; the launch traced here: 67.1 us
  Pallas kernels  66.3 us (98%)
  between operations  0.8 us (1%)
    pallas_call x1, Pallas kernels, shards(): pl.pallas_call(functools.partial(kernel, S, N, T, M, R, F, FA, chunks), o...  64.3 us
    pallas_call x1, Pallas kernels, shards(): pl.pallas_call(functools.partial(finish, unit, pl.ds(N * (RT - unit[2]),...  2.05 us

profile of v3, /device:TPU:0, one launch (start us, length us, event | category | flops | bytes accessed | tf_op | source)
XLA Modules:
  0.0 67.1 jit_solution(11744293234314825560)
XLA Ops:
  0.6 64.3 %shard_map.109 = (bf16[256,1024]{1,0:T(8,128)(2,1)S(1)}, bf16[256,1024]{1,0:T(8,128)(2,1)S(1)}, bf16[2,4,128,1024]{3,2,1,0:T(8,128)(2,1)S(1)}, bf16[1024,1024]{1...) custom-call(bf16[256,1024]{1,0:T(8,128)(2,1)} %bitcast.7, bf16[4,1024,1024]{2,1,0:T(8,128)(2,1)} %bitcast.6, ...), custom_call_target="tpu_custom_call" | custom-call | tf_op jit(solution)/shard_map/pallas_call | solution.py:704
  64.9 2.1 %shard_map.110 = (bf16[256,1024]{1,0:T(8,128)(2,1)}, bf16[256,1024]{1,0:T(8,128)(2,1)}, bf16[1024,1024]{1,0:T(8,128)(2,1)}, f32[1,16]{1,0:T(1,128)}, f32[1,16]{1,0:T(1,128)}, /*index=5*/f32[1,16]{1,0:T(1,128)}) custom-call(bf16[256,1024]{1,0:T(8,128)(2,1)S(1)} %get-tuple-element.18.acts, bf16[256,1024]{1,0:T(8,128)(2,1)S(1)} %get-tuple-element.19.grads, ...), custom_call_target="tpu_custom_call" | custom-call | tf_op jit(solution)/shard_map/pallas_call | solution.py:745
